TPU v7x, 32 devices: a whole 2x2x4 slice. The times are simulated.
32 devices in a mesh: probe: 4 (over x, core), fsdp: 8 (over z, y).
Axes of the slice: x: 2, y: 2, z: 4, core: 2. Of those that a mesh axis runs over, the one named last changes fastest.
Arguments:
- hidden: bfloat16 [16384, 2048], P(('probe', 'fsdp')), may hold values from -6 to 6
- norm_gain: bfloat16 [2048], replicated, may hold values from 0.5 to 1.5
- query_weight: bfloat16 [2048, 2048], P('fsdp'), may hold values from -1 to 1
- key_weight: bfloat16 [2048, 512], P('fsdp'), may hold values from -16 to 16
- value_weight: bfloat16 [2048, 512], P('fsdp'), may hold values from -0.125 to 0.125
- output_weight: bfloat16 [2048, 2048], P('fsdp'), may hold values from -0.125 to 0.125
- probe_seed: int32 [4], P('probe'), may hold values from 0 to 1073741823
Outputs:
- curvature_value: float32 [2048, 512], P('fsdp', 'probe')
- curvature_output: float32 [2048, 2048], P('fsdp', 'probe')
All inputs are finite; a program needn't handle non-finite values.
Results may differ from a plain program's by a relative error of at most 0.024.
Values may be sent and summed in bfloat16 or wider, within the bound.
A program may use at most 128 MiB of HBM per device.

v0:
```python
import functools
import heapq
import math

import jax
import jax.numpy as jnp
import numpy as np
from jax import lax
from jax.experimental import pallas as pl
from jax.experimental.pallas import tpu as pltpu
from jax.sharding import PartitionSpec as P

HEAD_DIM = 128
SEQ = 256
TILE = 256
MESH = pl.DeviceIdType.MESH
F32 = jnp.float32
BF16 = jnp.bfloat16

norm_eps = 1e-05
rope_base = 500000.0

MIX_A = 747796405
MIX_B = 668265261
MIX_C = 1274126177
MIX_SEED = 1664525
MIX_CODE = 374761393

ROWS_BY_ROWS = (((1,), (1,)), ((), ()))

US_PER_MB_ICI = 21.5
US_PER_MB_PAIR = 1.6
LATENCY_US = 2.0


def wrap32(value):
    value &= 0xFFFFFFFF
    return value - (1 << 32) if value >= (1 << 31) else value


def turn_tables():
    half = HEAD_DIM // 2
    position = np.arange(SEQ, dtype=np.float64)[:, None]
    angles = position * rope_base ** (-2.0 * np.arange(half, dtype=np.float64)[None] / HEAD_DIM)
    cosine, sine = np.cos(angles), np.sin(angles)
    return (
        np.concatenate([cosine, cosine], axis=1).astype(np.float32),
        np.concatenate([-sine, sine], axis=1).astype(np.float32),
    )


def bits_of(size):
    return [1 << place for place in range(size.bit_length() - 1)]


def low_bit(mask):
    return mask & -mask


def flip(index, mask):
    for bit in (1, 2, 4, 8, 16, 32, 64, 128):
        if mask & bit:
            index = index + bit - 2 * bit * lax.rem(lax.div(index, bit), 2)
    return index


def span(start, size):
    return pl.ds(pl.multiple_of(start, size), size)


class Plan:
    def __init__(self):
        self.now = 0.0
        self.arrivals = []
        self.tasks = []
        self.free = {}
        self.count = 0
        self.done = set()

    def post(self, link, us, action):
        start = max(self.now, self.free.get(link, 0.0))
        self.free[link] = start + us
        self.count += 1
        heapq.heappush(self.arrivals, (start + us + LATENCY_US, self.count, action))

    def task(self, name, us, needs, action):
        self.tasks.append((name, us, frozenset(needs), action))

    def run(self):
        while self.arrivals or self.tasks:
            if self.arrivals and self.arrivals[0][0] <= self.now:
                action = heapq.heappop(self.arrivals)[2]
                self.now += action() or 0.0
                continue
            ready = [entry for entry in self.tasks if entry[2] <= self.done]
            if ready:
                entry = ready[0]
                self.tasks.remove(entry)
                entry[3]()
                self.now += entry[1]
                self.done.add(entry[0])
                continue
            self.now = self.arrivals[0][0]


def stream_shapes(shards, rows, sizes, streams):
    shapes, sems = [], []
    for name, _, width, steps in streams:
        held, masks = 2, list(range(shards))
        for step in steps:
            if step == "x":
                held, slots = 1, list(masks)
            else:
                masks = [mask for mask in masks if not mask & step]
                slots = list(masks)
            shapes.append(((len(slots), rows, held * width), slots))
    return shapes


def layout(shards, tokens, width, query_width, key_width, probes):
    rows = width // shards
    q_part, k_part = query_width // probes, key_width // probes
    bits = bits_of(shards)
    near = bits[1:] if len(bits) > 1 else []
    streams = [
        ("a", 0, q_part // 2, ["x"] + bits),
        ("b", q_part, q_part // 2, bits[:1] + ["x"] + near),
        ("v", 0, k_part, near + bits[:1] + ["x"]),
    ]
    vm = lambda shape, kind=BF16: pltpu.VMEM(shape, kind)
    sem = lambda count: pltpu.SemaphoreType.DMA((count,))
    scratch = {
        "w": vm((probes, width, q_part + 2 * k_part)),
        "o": vm((query_width, width)),
        "hid": vm((tokens, width)),
        "normed": vm((tokens, width)),
        "sgn": vm((query_width, width)),
        "att": vm((probes * (tokens // SEQ) * (q_part // HEAD_DIM), SEQ, SEQ)),
        "tv": vm((tokens, key_width)),
        "raw": vm((tokens, q_part + 2 * k_part), F32),
        "cblk": vm((tokens, q_part)),
        "ctxt": vm((query_width, tokens)),
        "tctx": vm((tokens, query_width)),
        "acc": vm((tokens, width), F32),
        "bvt": vm((key_width, tokens)),
        "rxd": vm((shards, rows, 2 * q_part)),
        "rxdv": vm((shards, rows, 2 * k_part)),
        "local": sem(3 * probes + 2),
    }
    for kind in ("w", "x", "d1", "d3", "o", "od", "rd", "rdv"):
        scratch["send_" + kind] = sem(shards)
        scratch["recv_" + kind] = sem(shards)
    shapes = stream_shapes(shards, rows, None, streams)
    at = 0
    slots = {}
    for name, _, _, steps in streams:
        for step in range(len(steps)):
            shape, slot = shapes[at]
            at += 1
            scratch["rx_%s%d" % (name, step)] = vm(shape)
            scratch["send_%s%d" % (name, step)] = sem(shards)
            scratch["recv_%s%d" % (name, step)] = sem(len(slot))
            slots[name, step] = slot
    return scratch, streams, slots


def kernel(sizes, names, streams, slots, seed_ref, gain_ref, cos_ref, sin_ref, hid_in, q_in, k_in,
           v_in, o_in, value_out, output_out, *refs):
    shards, tokens, width, query_width, key_width, probes = sizes
    ref = dict(zip(names, refs))
    w, o, hid, normed, sgn, att = (ref[n] for n in ("w", "o", "hid", "normed", "sgn", "att"))
    tv, raw, cblk, ctxt, tctx, acc, bvt = (
        ref[n] for n in ("tv", "raw", "cblk", "ctxt", "tctx", "acc", "bvt")
    )
    cot = hid
    rows = width // shards
    q_part, k_part = query_width // probes, key_width // probes
    heads = q_part // HEAD_DIM
    sequences = tokens // SEQ
    out_half = width // 2
    bits = bits_of(shards)
    everyone = list(range(1, shards))

    pr = lax.axis_index("probe")
    fs = lax.axis_index("fsdp")
    core = lax.rem(pr, 2)
    block_of = [flip(pr, mask) for mask in range(probes)]
    shard_of = [flip(fs, mask) for mask in range(shards)]
    seed = seed_ref[0]
    plan = Plan()
    sent = []

    pair = {"probe": flip(pr, 1)}
    across = {"probe": flip(pr, 2)}
    along = {bit: {"fsdp": flip(fs, bit)} for bit in bits}

    def link_of(bit):
        return "y" if bit == bits[0] else "z"

    def push(kind, slot, source, target, device, receive_slot=None):
        copy = pltpu.make_async_remote_copy(
            src_ref=source,
            dst_ref=target,
            send_sem=ref["send_" + kind].at[slot],
            recv_sem=ref["recv_" + kind].at[slot if receive_slot is None else receive_slot],
            device_id=device,
            device_id_type=MESH,
        )
        copy.start()
        sent.append(copy)

    def arrived(kind, slot, target):
        pltpu.make_async_remote_copy(
            src_ref=target,
            dst_ref=target,
            send_sem=ref["send_" + kind].at[0],
            recv_sem=ref["recv_" + kind].at[slot],
            device_id=pair,
            device_id_type=MESH,
        ).wait_recv()

    def shard_rows(mask):
        return span(shard_of[mask] * rows, rows)

    def w_at(block, mask):
        return w.at[block, shard_rows(mask), :]

    def o_at(mask, half):
        return o.at[shard_rows(mask), span(half * out_half, out_half)]

    local = []

    def fetch(source, target):
        copy = pltpu.make_async_copy(source, target, ref["local"].at[len(local)])
        copy.start()
        local.append(copy)

    for block in range(probes):
        there = block_of[block]
        own = shard_rows(0)
        fetch(q_in.at[:, span(there * q_part, q_part)], w.at[block, own, 0:q_part])
        fetch(k_in.at[:, span(there * k_part, k_part)], w.at[block, own, q_part : q_part + k_part])
        fetch(
            v_in.at[:, span(there * k_part, k_part)],
            w.at[block, own, q_part + k_part : q_part + 2 * k_part],
        )
    fetch(o_in, o.at[shard_rows(0), :])
    fetch(hid_in, hid)

    barrier = pltpu.get_barrier_semaphore()
    greeted = [pair, across] + [along[bit] for bit in bits]
    for device in greeted:
        pl.semaphore_signal(barrier, inc=1, device_id=device, device_id_type=MESH)
    pl.semaphore_wait(barrier, len(greeted))

    w_mb = rows * (q_part + 2 * k_part) * 2e-6
    o_mb = rows * out_half * 2e-6
    left = {"w": set(everyone), "x": set(everyone), "o": set(everyone)}

    def finish(kind, mask):
        left[kind].discard(mask)
        if not left[kind]:
            plan.done.add("all_" + kind)

    def ici_us(bit, size_mb):
        return size_mb * US_PER_MB_ICI * (2.0 if bit > 2 else 1.0)

    def send_w(mask, bit):
        got = mask ^ bit
        push("w", got, w_at(0, mask), w_at(0, mask), along[bit])
        plan.post(link_of(bit), ici_us(bit, w_mb), lambda: got_w(got))

    far_masks = {mask for mask in everyone if low_bit(mask) > 2}

    def got_w(mask):
        arrived("w", mask, w_at(0, mask))
        for bit in reversed(bits):
            if bit < low_bit(mask):
                send_w(mask, bit)
        push("x", mask, w_at(0, mask), w_at(2, mask), across)
        plan.post("x", w_mb * US_PER_MB_ICI, lambda: got_x(mask))
        push("d1", mask, w_at(0, mask), w_at(1, mask), pair)
        finish("w", mask)
        if mask in far_masks:
            far_masks.discard(mask)
            if not far_masks:
                start_far_o()

    def got_x(mask):
        arrived("x", mask, w_at(2, mask))
        push("d3", mask, w_at(2, mask), w_at(3, mask), pair)
        finish("x", mask)

    def send_o(mask, bit):
        got = mask ^ bit
        push("o", got, o_at(mask, core), o_at(mask, core), along[bit])
        plan.post(link_of(bit), ici_us(bit, o_mb), lambda: got_o(got))

    def got_o(mask):
        arrived("o", mask, o_at(mask, core))
        for bit in reversed(bits):
            if bit < low_bit(mask):
                send_o(mask, bit)
        push("od", mask, o_at(mask, core), o_at(mask, core), pair)
        finish("o", mask)

    def start_far_o():
        for bit in reversed(bits[1:]):
            send_o(0, bit)

    for copy in local[:3]:
        copy.wait()
    for bit in reversed(bits):
        send_w(0, bit)
    for copy in local[3:]:
        copy.wait()
    send_o(0, bits[0])
    if not far_masks:
        start_far_o()

    def normalize():
        gain = gain_ref[...].astype(F32)

        def step(index, carry):
            part = span(index * 16, 16)
            values = hid[part, :].astype(F32)
            inverse = lax.rsqrt(jnp.mean(values * values, axis=1, keepdims=True) + norm_eps)
            normed[part, :] = (values * inverse * gain).astype(BF16)
            return carry

        lax.fori_loop(0, tokens // 16, step, 0)

    def signs(offset, columns, shape):
        spread = (
            lax.broadcasted_iota(jnp.int32, shape, 0) * columns
            + lax.broadcasted_iota(jnp.int32, shape, 1)
        ) * MIX_A

        def at(start):
            mixed = spread + (start * MIX_A + offset)
            mixed = mixed ^ lax.shift_right_logical(mixed, jnp.int32(15))
            mixed = mixed * MIX_B
            mixed = mixed ^ lax.shift_right_logical(mixed, jnp.int32(13))
            mixed = mixed * MIX_C
            mixed = mixed ^ lax.shift_right_logical(mixed, jnp.int32(16))
            return jnp.where((mixed & 1) == 1, 1.0, -1.0).astype(BF16)

        return at

    deep = width // TILE

    def value_signs(column):
        make = signs(seed * MIX_SEED, key_width, (32, TILE))
        per = TILE // 32

        def step(index, carry):
            tile, part = lax.div(index, per), lax.rem(index, per)
            start = index * 32 * key_width + column * TILE
            att[column * deep + tile, span(part * 32, 32), :] = make(start)
            return carry

        lax.fori_loop(0, width // 32, step, 0)

    def tangent():
        for column in range(key_width // TILE):
            table = att[column * deep : (column + 1) * deep].reshape(width, TILE)
            product = jnp.dot(normed[...], table, preferred_element_type=F32)
            tv[:, column * TILE : (column + 1) * TILE] = (product * width ** (-0.5)).astype(BF16)

    sign_parts = 8

    def out_signs(part):
        make = signs(seed * MIX_SEED + MIX_CODE, width, (16, 512))
        depth = query_width // sign_parts

        def step(index, carry):
            row = part * depth + index * 16
            for column in range(0, width, 512):
                sgn[span(row, 16), column : column + 512] = make(row * width + column)
            return carry

        lax.fori_loop(0, depth // 16, step, 0)

    def project(block):
        if block == 1:
            for mask in everyone:
                arrived("d1", mask, w_at(1, mask))
        if block == 3:
            for mask in everyone:
                arrived("d3", mask, w_at(3, mask))

        def step(index, carry):
            part = span(index * TILE, TILE)
            raw[:, part] = jnp.dot(normed[...], w[block, :, part], preferred_element_type=F32)
            return carry

        lax.fori_loop(0, (q_part + 2 * k_part) // TILE, step, 0)

    mask_shape = (SEQ, SEQ)

    def attend(block):
        there = block_of[block]
        seen = lax.broadcasted_iota(jnp.int32, mask_shape, 0) >= lax.broadcasted_iota(
            jnp.int32, mask_shape, 1
        )
        factor = math.log2(math.e) * HEAD_DIM ** (-0.5)

        def step(sequence, carry):
            part = span(sequence * SEQ, SEQ)
            cosine, sine = cos_ref[...], sin_ref[...]

            def turned(low):
                piece = raw[part, low : low + HEAD_DIM]
                other = pltpu.roll(piece, HEAD_DIM // 2, 1)
                return (piece * cosine + other * sine).astype(BF16)

            key = turned(q_part)
            value = raw[part, q_part + k_part : q_part + 2 * k_part].astype(BF16)
            both = jnp.concatenate([value, tv[part, span(there * k_part, k_part)]], axis=1)
            for head in range(heads):
                low = head * HEAD_DIM
                scores = lax.dot_general(
                    turned(low), key, ROWS_BY_ROWS, preferred_element_type=F32
                )
                scores = jnp.where(seen, scores, -1e30)
                raised = jnp.exp2((scores - jnp.max(scores, axis=1, keepdims=True)) * factor)
                share = 1.0 / jnp.sum(raised, axis=1, keepdims=True)
                weight = (raised * share).astype(BF16)
                att[block * sequences * heads + sequence * heads + head] = weight
                mixed = jnp.dot(weight, both, preferred_element_type=F32)
                first = mixed[:, :HEAD_DIM]
                cblk[part, low : low + HEAD_DIM] = first.astype(BF16)
                ctxt[span(there * q_part + low, HEAD_DIM), part] = first.T.astype(BF16)
                tctx[part, span(there * q_part + low, HEAD_DIM)] = mixed[:, HEAD_DIM:].astype(BF16)
            return carry

        lax.fori_loop(0, sequences, step, 0)

    def probe(block):
        there = block_of[block]

        def step(index, carry):
            part = span(index * TILE, TILE)
            product = jnp.dot(
                cblk[...], sgn[span(there * q_part, q_part), part], preferred_element_type=F32
            )
            acc[:, part] = product if block == 0 else acc[:, part] + product
            return carry

        lax.fori_loop(0, width // TILE, step, 0)

    def transpose_normed():
        for copy in sent:
            copy.wait_send()
        sent.clear()

        def step(index, carry):
            part = span(index * 128, 128)
            w[0, part, 0:tokens] = normed[:, part].astype(F32).T.astype(BF16)
            return carry

        lax.fori_loop(0, width // 128, step, 0)

    def forward():
        for mask in everyone:
            arrived("od", mask, o_at(mask, 1 - core))

        def step(index, carry):
            part = span(index * TILE, TILE)
            product = jnp.dot(tctx[...], o[:, part], preferred_element_type=F32)
            cot[:, part] = (product + acc[:, part] * query_width ** (-0.5)).astype(BF16)
            return carry

        lax.fori_loop(0, width // TILE, step, 0)

    def back_context(block):
        def step(index, carry):
            part = span(index * SEQ, SEQ)
            w[2, block * q_part : (block + 1) * q_part, part] = lax.dot_general(
                o[span(block_of[block] * q_part, q_part), :],
                cot[part, :],
                ROWS_BY_ROWS,
                preferred_element_type=F32,
            ).astype(BF16)
            return carry

        lax.fori_loop(0, sequences, step, 0)

    place_of = {0: 0, 2: 1, 1: 2, 3: 3}

    def spread_back(block):
        def step(sequence, carry):
            part = span(sequence * SEQ, SEQ)
            total = jnp.zeros((HEAD_DIM, SEQ), F32)
            for head in range(heads):
                low = block * q_part + head * HEAD_DIM
                total = total + jnp.dot(
                    w[2, low : low + HEAD_DIM, part],
                    att[block * sequences * heads + sequence * heads + head],
                    preferred_element_type=F32,
                )
            low = place_of[block] * HEAD_DIM
            bvt[low : low + HEAD_DIM, part] = total.astype(BF16)
            return carry

        lax.fori_loop(0, sequences, step, 0)

    def add(read_a, read_b, write, wide):
        chunk = max(16, min(rows, 16384 // wide))

        def step(index, carry):
            part = span(index * chunk, chunk)
            write(part, read_a(part).astype(F32) + read_b(part).astype(F32))
            return carry

        lax.fori_loop(0, rows // chunk, step, 0)
        return rows * wide * 1.5e-6

    table = {}
    for name, base, wide, steps in streams:
        table[name] = (base, wide, steps, set(), set())

    def home(name, mask, low, wide):
        part = slice(mask * rows, (mask + 1) * rows)
        if name == "v":
            return w.at[1, part, low : low + wide]
        return sgn.at[part, low : low + wide]

    def ready(name, step, mask):
        base, wide, steps, waiting, landed = table[name]
        act = steps[step]
        held = 1 if "x" in steps[:step] else 2
        kind = "%s%d" % (name, step)
        inbox = ref["rx_" + kind]
        if act == "x":
            slot = slots[name, step].index(mask)
            push(kind, mask, home(name, mask, base + wide, wide), inbox.at[slot], across, slot)
            plan.post("x", rows * wide * 2e-6 * US_PER_MB_ICI, lambda: land(name, step, mask))
            waiting.add((step, mask))
            return 0.0
        if mask & act:
            got = mask ^ act
            slot = slots[name, step].index(got)
            push(kind, mask, home(name, mask, base, held * wide), inbox.at[slot], along[act], slot)
            plan.post(
                link_of(act),
                ici_us(act, rows * held * wide * 2e-6),
                lambda: land(name, step, got),
            )
            return 0.0
        waiting.add((step, mask))
        return combine(name, step, mask)

    def land(name, step, mask):
        table[name][4].add((step, mask))
        return combine(name, step, mask)

    def combine(name, step, mask):
        base, wide, steps, waiting, landed = table[name]
        if (step, mask) not in waiting or (step, mask) not in landed:
            return 0.0
        held = 1 if "x" in steps[: step + 1] else 2
        kind = "%s%d" % (name, step)
        slot = slots[name, step].index(mask)
        inbox = ref["rx_" + kind]
        arrived(kind, slot, inbox.at[slot])
        mine = home(name, mask, base, held * wide)
        last = step + 1 == len(steps)

        def write(part, total):
            if not last:
                mine[part, :] = total.astype(BF16)
            elif name == "v":
                value_out[part, :] = total
            elif name == "a":
                output_out[part, 0:wide] = total
            else:
                output_out[part, wide : 2 * wide] = total

        us = add(lambda p: mine[p, :], lambda p: inbox[slot, p, :], write, held * wide)
        return us if last else us + ready(name, step + 1, mask)

    def out_term(mask):
        left_part = ctxt[shard_rows(mask), :]
        target = slice(mask * rows, (mask + 1) * rows)
        piece = q_part // 2

        def step(index, carry):
            other, half, far = lax.div(index, 4), lax.rem(lax.div(index, 2), 2), lax.rem(index, 2)
            mine_core, mine_far = lax.rem(pr, 2), lax.div(pr, 2)
            block = (mine_far + far - 2 * mine_far * far) * 2 + (
                mine_core + other - 2 * mine_core * other
            )
            columns = span(block * q_part + half * piece, piece)
            sgn[target, span(index * piece, piece)] = jnp.dot(
                left_part, cot[:, columns], preferred_element_type=F32
            ).astype(BF16)
            return carry

        lax.fori_loop(0, width // piece, step, 0)
        push("rd", mask, home("a", mask, 2 * q_part, 2 * q_part), ref["rxd"].at[mask], pair)

        def met():
            arrived("rd", mask, ref["rxd"].at[mask])
            mine = home("a", mask, 0, 2 * q_part)

            def write(part, total):
                mine[part, :] = total.astype(BF16)

            us = add(lambda p: mine[p, :], lambda p: ref["rxd"][mask, p, :], write, 2 * q_part)
            us += ready("b", 0, mask)
            return us + ready("a", 0, mask)

        plan.post("pair", rows * 2 * q_part * 2e-6 * US_PER_MB_PAIR, met)

    def value_term(mask):
        target = slice(mask * rows, (mask + 1) * rows)
        w[1, target, 0:key_width] = lax.dot_general(
            w[0, shard_rows(mask), 0:tokens], bvt[...], ROWS_BY_ROWS, preferred_element_type=F32
        ).astype(BF16)
        push("rdv", mask, home("v", mask, 2 * k_part, 2 * k_part), ref["rxdv"].at[mask], pair)

        def met():
            arrived("rdv", mask, ref["rxdv"].at[mask])
            mine = home("v", mask, 0, 2 * k_part)

            def write(part, total):
                mine[part, :] = total.astype(BF16)

            us = add(lambda p: mine[p, :], lambda p: ref["rxdv"][mask, p, :], write, 2 * k_part)
            return us + ready("v", 0, mask)

        plan.post("pair", rows * 2 * k_part * 2e-6 * US_PER_MB_PAIR, met)

    plan.task("norm", 1.5, (), normalize)
    for column in range(key_width // TILE):
        plan.task("value_signs%d" % column, 1.3, (), functools.partial(value_signs, column))
    sign_names = ["value_signs%d" % column for column in range(key_width // TILE)]
    plan.task("tangent", 1.5, ["norm"] + sign_names, tangent)
    for part in range(sign_parts):
        plan.task("out_signs%d" % part, 1.2, (), functools.partial(out_signs, part))
    sign_names = ["out_signs%d" % part for part in range(sign_parts)]
    before = ["tangent"] + sign_names
    for block in range(probes):
        arrival = "all_w" if block < 2 else "all_x"
        plan.task("project%d" % block, 2.5, before + [arrival], functools.partial(project, block))
        plan.task("attend%d" % block, 4.2, ["project%d" % block], functools.partial(attend, block))
        plan.task("probe%d" % block, 1.7, ["attend%d" % block], functools.partial(probe, block))
        before = ["probe%d" % block]
    plan.task("turn", 1.0, before + ["all_o"], transpose_normed)
    plan.task("forward", 5.0, ["turn"], forward)
    out_order = sorted(range(shards), key=lambda mask: [-(mask & bit) for bit in bits])
    value_order = sorted(range(shards), key=lambda mask: [-(mask & b) for b in bits[1:] + bits[:1]])
    terms = [("out%d" % mask, 0.9, ("forward",), functools.partial(out_term, mask)) for mask in out_order]
    chain = []
    for block in range(probes):
        chain.append(("back%d" % block, 1.5, ("forward",), functools.partial(back_context, block)))
        chain.append(
            ("spread%d" % block, 1.0, ("back%d" % block,), functools.partial(spread_back, block))
        )
    spread_names = ["spread%d" % block for block in range(probes)]
    values = [
        ("value%d" % mask, 0.2, spread_names, functools.partial(value_term, mask))
        for mask in value_order
    ]
    merged, early = [], 2
    merged += terms[:early]
    rest = terms[early:]
    while rest or chain:
        merged += chain[:1]
        merged += rest[:1]
        chain, rest = chain[1:], rest[1:]
    for entry in merged + values:
        plan.task(*entry)
    plan.run()
    for copy in sent:
        copy.wait_send()


def body(hidden, norm_gain, query_weight, key_weight, value_weight, output_weight, probe_seed):
    tokens, width = hidden.shape
    query_width, key_width = query_weight.shape[1], key_weight.shape[1]
    probes, shards = lax.axis_size("probe"), lax.axis_size("fsdp")
    sizes = (shards, tokens, width, query_width, key_width, probes)
    assert probes == 4 and key_width == probes * HEAD_DIM and width == query_width
    scratch, streams, slots = layout(*sizes)
    cosine, sine = turn_tables()
    vmem = pl.BlockSpec(memory_space=pltpu.VMEM)
    anywhere = pl.BlockSpec(memory_space=pl.ANY)
    rows = width // shards
    return pl.pallas_call(
        functools.partial(kernel, sizes, list(scratch), streams, slots),
        in_specs=[pl.BlockSpec(memory_space=pltpu.SMEM)] + [vmem] * 3 + [anywhere] * 5,
        out_specs=[vmem, vmem],
        out_shape=[
            jax.ShapeDtypeStruct((rows, key_width // probes), F32),
            jax.ShapeDtypeStruct((rows, width // probes), F32),
        ],
        scratch_shapes=list(scratch.values()),
        compiler_params=pltpu.CompilerParams(
            collective_id=0, has_side_effects=True, vmem_limit_bytes=67043328
        ),
    )(
        probe_seed,
        norm_gain.reshape(1, width),
        jnp.asarray(cosine),
        jnp.asarray(sine),
        hidden,
        query_weight,
        key_weight,
        value_weight,
        output_weight,
    )


def solution(mesh):
    return jax.shard_map(
        body,
        mesh=mesh,
        in_specs=(
            P(("probe", "fsdp"), None),
            P(),
            P("fsdp", None),
            P("fsdp", None),
            P("fsdp", None),
            P("fsdp", None),
            P("probe"),
        ),
        out_specs=(P("fsdp", "probe"), P("fsdp", "probe")),
        check_vma=False,
    )
```

profile of v0, /device:TPU:0, one launch (start us, length us, event | category | flops | bytes accessed | tf_op | source)
XLA Modules:
  0.0 185.2 jit_solution(8025771387132933624)
XLA Ops:
  1.3 1.3 reshape.7.gain_ref
  2.6 179.2 %shard_map.104 = (f32[256,128]{1,0:T(8,128)}, f32[256,512]{1,0:T(8,128)}) custom-call(s32[1]{0:T(128)S(6)} %copy.13.seed_ref, bf16[1,2048]{1,0:T(2,128)(2,1)} %reshape.7.gain_ref, f32[256,128]{1,0:T(8,128)} %constant.4.clone.cos_ref, f32[256,128]{1,0:T(8,128)} %constant.5.clone.sin_ref, bf16[512,2048]{1,0:T(8,128)(2,1)} %hid_in.1, bf16[256,2048]{1,0:T(8,128)(2,1)} %q_in.1, ...), custom_call_target="tpu_custom_call" | custom-call | tf_op jit(solution)/shard_map/pallas_call | solution.py:691
  181.8 1.6 copy.14
  183.3 1.9 %copy.15 = f32[256,512]{1,0:T(8,128)} copy(f32[256,512]{1,0:T(8,128)} %get-tuple-element.5) | data formatting | bytes 1048576
where the time goes:
time: 185 us
  Pallas kernels  179 us (97%)
  local copies, waits for them, and re-layouts  4.73 us (3%)
    pallas_call x1, Pallas kernels, body(): pl.pallas_call(functools.partial(kernel, sizes, list(scratch), streams, s...  179 us

commit v1 on v0

--- a/solution.py
+++ b/solution.py
@@ -31,6 +31,8 @@
 US_PER_MB_ICI = 21.5
 US_PER_MB_PAIR = 1.6
 LATENCY_US = 2.0
+AHEAD_US = 5.0
+PARTS = 2
 
 
 def wrap32(value):
@@ -64,43 +66,59 @@
     return index
 
 
-def span(start, size):
-    return pl.ds(pl.multiple_of(start, size), size)
+def span(start, unit, size=None):
+    return pl.ds(pl.multiple_of(start, unit), unit if size is None else size)
 
 
 class Plan:
     def __init__(self):
         self.now = 0.0
         self.arrivals = []
+        self.waiting = {}
         self.tasks = []
         self.free = {}
         self.count = 0
         self.done = set()
 
-    def post(self, link, us, action):
-        start = max(self.now, self.free.get(link, 0.0))
-        self.free[link] = start + us
+    def post(self, name, link, us, rank, start, action, slow=1.0):
         self.count += 1
-        heapq.heappush(self.arrivals, (start + us + LATENCY_US, self.count, action))
+        heap = self.waiting.setdefault(link, [])
+        heapq.heappush(heap, (rank, self.count, name, us, slow, start, action))
+        self.pump()
+
+    def pump(self):
+        for link, heap in self.waiting.items():
+            while heap and self.free.get(link, 0.0) <= self.now + AHEAD_US:
+                rank, count, name, us, slow, start, action = heapq.heappop(heap)
+                begin = max(self.now, self.free.get(link, 0.0))
+                self.free[link] = begin + us
+                start()
+                due = begin + us * slow + LATENCY_US
+                heapq.heappush(self.arrivals, (due, count, name, action))
 
     def task(self, name, us, needs, action):
         self.tasks.append((name, us, frozenset(needs), action))
 
     def run(self):
-        while self.arrivals or self.tasks:
+        while self.arrivals or self.tasks or any(self.waiting.values()):
+            self.pump()
             if self.arrivals and self.arrivals[0][0] <= self.now:
-                action = heapq.heappop(self.arrivals)[2]
-                self.now += action() or 0.0
+                name, action = heapq.heappop(self.arrivals)[2:]
+                with jax.named_scope(name):
+                    self.now += action() or 0.0
                 continue
             ready = [entry for entry in self.tasks if entry[2] <= self.done]
             if ready:
                 entry = ready[0]
                 self.tasks.remove(entry)
-                entry[3]()
+                with jax.named_scope(entry[0]):
+                    entry[3]()
                 self.now += entry[1]
                 self.done.add(entry[0])
                 continue
-            self.now = self.arrivals[0][0]
+            times = [self.free[link] - AHEAD_US for link, heap in self.waiting.items() if heap]
+            times += [entry[0] for entry in self.arrivals[:1]]
+            self.now = max(self.now, min(times)) + 1e-6
 
 
 def stream_shapes(shards, rows, sizes, streams):
@@ -137,8 +155,8 @@
         "sgn": vm((query_width, width)),
         "att": vm((probes * (tokens // SEQ) * (q_part // HEAD_DIM), SEQ, SEQ)),
         "tv": vm((tokens, key_width)),
-        "raw": vm((tokens, q_part + 2 * k_part), F32),
-        "cblk": vm((tokens, q_part)),
+        "raw": vm((2, tokens, q_part + 2 * k_part), F32),
+        "cblk": vm((probes, tokens, q_part)),
         "ctxt": vm((query_width, tokens)),
         "tctx": vm((tokens, query_width)),
         "acc": vm((tokens, width), F32),
@@ -147,9 +165,9 @@
         "rxdv": vm((shards, rows, 2 * k_part)),
         "local": sem(3 * probes + 2),
     }
-    for kind in ("w", "x", "d1", "d3", "o", "od", "rd", "rdv"):
-        scratch["send_" + kind] = sem(shards)
-        scratch["recv_" + kind] = sem(shards)
+    for kind in ("w", "x", "d1", "d3", "f", "fd", "e", "ed", "rd", "rdv"):
+        scratch["send_" + kind] = sem(shards * PARTS)
+        scratch["recv_" + kind] = sem(shards * PARTS)
     shapes = stream_shapes(shards, rows, None, streams)
     at = 0
     slots = {}
@@ -188,7 +206,7 @@
     shard_of = [flip(fs, mask) for mask in range(shards)]
     seed = seed_ref[0]
     plan = Plan()
-    sent = []
+    sent = {}
 
     pair = {"probe": flip(pr, 1)}
     across = {"probe": flip(pr, 2)}
@@ -207,7 +225,12 @@
             device_id_type=MESH,
         )
         copy.start()
-        sent.append(copy)
+        sent.setdefault(kind, []).append(copy)
+
+    def drain(kinds):
+        for kind in kinds:
+            for copy in sent.pop(kind, []):
+                copy.wait_send()
 
     def arrived(kind, slot, target):
         pltpu.make_async_remote_copy(
@@ -219,14 +242,25 @@
             device_id_type=MESH,
         ).wait_recv()
 
+    part_rows = rows // PARTS
+
     def shard_rows(mask):
         return span(shard_of[mask] * rows, rows)
 
-    def w_at(block, mask):
-        return w.at[block, shard_rows(mask), :]
-
-    def o_at(mask, half):
-        return o.at[shard_rows(mask), span(half * out_half, out_half)]
+    def piece_rows(mask, part):
+        return span(shard_of[mask] * rows + part * part_rows, part_rows)
+
+    def w_at(block, mask, part):
+        return w.at[block, piece_rows(mask, part), :]
+
+    early_lanes = out_half // 4
+
+    def f_at(half, mask, part):
+        lanes = span(half * out_half + early_lanes, early_lanes, out_half - early_lanes)
+        return o.at[piece_rows(mask, part), lanes]
+
+    def e_at(half, mask, part):
+        return o.at[shard_rows(mask), span(half * out_half, early_lanes)]
 
     local = []
 
@@ -244,8 +278,9 @@
             v_in.at[:, span(there * k_part, k_part)],
             w.at[block, own, q_part + k_part : q_part + 2 * k_part],
         )
-    fetch(o_in, o.at[shard_rows(0), :])
-    fetch(hid_in, hid)
+        if block == 0:
+            fetch(hid_in, hid)
+            fetch(o_in, o.at[shard_rows(0), :])
 
     barrier = pltpu.get_barrier_semaphore()
     greeted = [pair, across] + [along[bit] for bit in bits]
@@ -253,72 +288,113 @@
         pl.semaphore_signal(barrier, inc=1, device_id=device, device_id_type=MESH)
     pl.semaphore_wait(barrier, len(greeted))
 
-    w_mb = rows * (q_part + 2 * k_part) * 2e-6
-    o_mb = rows * out_half * 2e-6
-    left = {"w": set(everyone), "x": set(everyone), "o": set(everyone)}
-
-    def finish(kind, mask):
-        left[kind].discard(mask)
+    left = {}
+
+    def finish(kind, mask, part):
+        left[kind].discard((mask, part))
+        if not any(key[0] == mask for key in left[kind]):
+            plan.done.add("%s%d" % (kind, mask))
         if not left[kind]:
             plan.done.add("all_" + kind)
 
-    def ici_us(bit, size_mb):
-        return size_mb * US_PER_MB_ICI * (2.0 if bit > 2 else 1.0)
-
-    def send_w(mask, bit):
-        got = mask ^ bit
-        push("w", got, w_at(0, mask), w_at(0, mask), along[bit])
-        plan.post(link_of(bit), ici_us(bit, w_mb), lambda: got_w(got))
-
-    far_masks = {mask for mask in everyone if low_bit(mask) > 2}
-
-    def got_w(mask):
-        arrived("w", mask, w_at(0, mask))
-        for bit in reversed(bits):
-            if bit < low_bit(mask):
-                send_w(mask, bit)
-        push("x", mask, w_at(0, mask), w_at(2, mask), across)
-        plan.post("x", w_mb * US_PER_MB_ICI, lambda: got_x(mask))
-        push("d1", mask, w_at(0, mask), w_at(1, mask), pair)
-        finish("w", mask)
-        if mask in far_masks:
-            far_masks.discard(mask)
-            if not far_masks:
-                start_far_o()
-
-    def got_x(mask):
-        arrived("x", mask, w_at(2, mask))
-        push("d3", mask, w_at(2, mask), w_at(3, mask), pair)
-        finish("x", mask)
-
-    def send_o(mask, bit):
-        got = mask ^ bit
-        push("o", got, o_at(mask, core), o_at(mask, core), along[bit])
-        plan.post(link_of(bit), ici_us(bit, o_mb), lambda: got_o(got))
-
-    def got_o(mask):
-        arrived("o", mask, o_at(mask, core))
-        for bit in reversed(bits):
-            if bit < low_bit(mask):
-                send_o(mask, bit)
-        push("od", mask, o_at(mask, core), o_at(mask, core), pair)
-        finish("o", mask)
-
-    def start_far_o():
-        for bit in reversed(bits[1:]):
-            send_o(0, bit)
-
+    def hand_over(kind, mask, part, source, target):
+        slot = mask * PARTS + part
+        plan.post(
+            "%s_%d_%d" % (kind, mask, part),
+            "pair",
+            size_mb(source) * US_PER_MB_PAIR,
+            0,
+            lambda: push(kind, slot, source, target, pair),
+            lambda: finish(kind, mask, part),
+        )
+
+    def size_mb(piece):
+        return math.prod(piece.shape) * 2e-6
+
+    def channel(kind, order, rank, place, parts, then):
+        pieces = {(mask, part) for mask in everyone for part in range(parts)}
+        left[kind] = set(pieces)
+
+        def send(mask, part, bit):
+            got = mask ^ bit
+            here = place(mask, part)
+            plan.post(
+                "%s_%d_%d" % (kind, got, part),
+                link_of(bit),
+                size_mb(here) * US_PER_MB_ICI,
+                (0.5 if kind == "e" and bit == bits[0] else rank, order.index(bit)),
+                lambda: push(kind, got * PARTS + part, here, here, along[bit]),
+                lambda: take(got, part),
+                2.0 if bit > 2 else 1.0,
+            )
+
+        def onward(mask, part, only=None):
+            last = max([order.index(bit) for bit in bits if mask & bit], default=-1)
+            for bit in order[last + 1 :]:
+                if only is None or bit in only:
+                    send(mask, part, bit)
+
+        def take(mask, part):
+            arrived(kind, mask * PARTS + part, place(mask, part))
+            onward(mask, part)
+            then(mask, part)
+            finish(kind, mask, part)
+
+        return onward
+
+    left["x"] = {(mask, part) for mask in everyone for part in range(PARTS)}
+    for kind in ("d1", "d3", "fd"):
+        left[kind] = set(left["x"])
+    left["ed"] = {(mask, 0) for mask in everyone}
+
+    first_wave = {(mask, part) for mask in everyone[1::2] for part in range(PARTS)}
+
+    def after_w(mask, part):
+        here = w_at(0, mask, part)
+        first_wave.discard((mask, part))
+        if not first_wave and not second_wave:
+            second_wave.append(True)
+            for piece in range(PARTS):
+                start_f(0, piece, bits[1:])
+            start_e(0, 0, bits[1:])
+
+        def got_x():
+            arrived("x", mask * PARTS + part, w_at(2, mask, part))
+            hand_over("d3", mask, part, w_at(2, mask, part), w_at(3, mask, part))
+            finish("x", mask, part)
+
+        plan.post(
+            "x_%d_%d" % (mask, part),
+            "x",
+            size_mb(here) * US_PER_MB_ICI,
+            0,
+            lambda: push("x", mask * PARTS + part, here, w_at(2, mask, part), across),
+            got_x,
+        )
+        hand_over("d1", mask, part, here, w_at(1, mask, part))
+
+    def after_f(mask, part):
+        hand_over("fd", mask, part, f_at(core, mask, part), f_at(core, mask, part))
+
+    def after_e(mask, part):
+        hand_over("ed", mask, part, e_at(core, mask, part), e_at(core, mask, part))
+
+    start_w = channel("w", bits[::-1], 0, functools.partial(w_at, 0), PARTS, after_w)
+    start_f = channel("f", bits[::-1], 1, functools.partial(f_at, core), PARTS, after_f)
+    start_e = channel("e", bits[:1] + bits[:0:-1], 2, functools.partial(e_at, core), 1, after_e)
+
+    second_wave = []
     for copy in local[:3]:
         copy.wait()
-    for bit in reversed(bits):
-        send_w(0, bit)
-    for copy in local[3:]:
-        copy.wait()
-    send_o(0, bits[0])
-    if not far_masks:
-        start_far_o()
+    for part in range(PARTS):
+        start_w(0, part)
+    local[4].wait()
+    start_e(0, 0, bits[:1])
+    for part in range(PARTS):
+        start_f(0, part, bits[:1])
 
     def normalize():
+        local[3].wait()
         gain = gain_ref[...].astype(F32)
 
         def step(index, carry):
@@ -382,16 +458,39 @@
         lax.fori_loop(0, depth // 16, step, 0)
 
     def project(block):
-        if block == 1:
-            for mask in everyone:
-                arrived("d1", mask, w_at(1, mask))
-        if block == 3:
-            for mask in everyone:
-                arrived("d3", mask, w_at(3, mask))
-
         def step(index, carry):
             part = span(index * TILE, TILE)
-            raw[:, part] = jnp.dot(normed[...], w[block, :, part], preferred_element_type=F32)
+            raw[block % 2, :, part] = jnp.dot(
+                normed[...], w[block, :, part], preferred_element_type=F32
+            )
+            return carry
+
+        lax.fori_loop(0, (q_part + 2 * k_part) // TILE, step, 0)
+
+    def bring(block, masks):
+        if 0 in masks and block:
+            for copy in local[2 + 3 * block : 5 + 3 * block]:
+                copy.wait()
+        if block % 2:
+            for mask in masks:
+                for part in range(PARTS if mask else 0):
+                    arrived(flags[block], mask * PARTS + part, w_at(block, mask, part))
+
+    def whole_project(block):
+        bring(block, range(shards))
+        project(block)
+
+    def add_shards(block, masks, first):
+        bring(block, masks)
+        cut = [normed[:, shard_rows(mask)] for mask in masks]
+        left_part = jnp.concatenate(cut, axis=1) if len(cut) > 1 else cut[0]
+
+        def step(index, carry):
+            part = span(index * TILE, TILE)
+            cut = [w[block, shard_rows(mask), part] for mask in masks]
+            right_part = jnp.concatenate(cut, axis=0) if len(cut) > 1 else cut[0]
+            product = jnp.dot(left_part, right_part, preferred_element_type=F32)
+            raw[block % 2, :, part] = product if first else raw[block % 2, :, part] + product
             return carry
 
         lax.fori_loop(0, (q_part + 2 * k_part) // TILE, step, 0)
@@ -410,12 +509,12 @@
             cosine, sine = cos_ref[...], sin_ref[...]
 
             def turned(low):
-                piece = raw[part, low : low + HEAD_DIM]
+                piece = raw[block % 2, part, low : low + HEAD_DIM]
                 other = pltpu.roll(piece, HEAD_DIM // 2, 1)
                 return (piece * cosine + other * sine).astype(BF16)
 
             key = turned(q_part)
-            value = raw[part, q_part + k_part : q_part + 2 * k_part].astype(BF16)
+            value = raw[block % 2, part, q_part + k_part : q_part + 2 * k_part].astype(BF16)
             both = jnp.concatenate([value, tv[part, span(there * k_part, k_part)]], axis=1)
             for head in range(heads):
                 low = head * HEAD_DIM
@@ -429,31 +528,28 @@
                 att[block * sequences * heads + sequence * heads + head] = weight
                 mixed = jnp.dot(weight, both, preferred_element_type=F32)
                 first = mixed[:, :HEAD_DIM]
-                cblk[part, low : low + HEAD_DIM] = first.astype(BF16)
+                cblk[block, part, low : low + HEAD_DIM] = first.astype(BF16)
                 ctxt[span(there * q_part + low, HEAD_DIM), part] = first.T.astype(BF16)
                 tctx[part, span(there * q_part + low, HEAD_DIM)] = mixed[:, HEAD_DIM:].astype(BF16)
             return carry
 
         lax.fori_loop(0, sequences, step, 0)
 
-    def probe(block):
-        there = block_of[block]
-
+    def probe_product(blocks, part):
+        left_part = jnp.concatenate([cblk[block] for block in blocks], axis=1)
+        cut = [sgn[span(block_of[block] * q_part, q_part), part] for block in blocks]
+        return jnp.dot(left_part, jnp.concatenate(cut, axis=0), preferred_element_type=F32)
+
+    def probe(blocks):
         def step(index, carry):
             part = span(index * TILE, TILE)
-            product = jnp.dot(
-                cblk[...], sgn[span(there * q_part, q_part), part], preferred_element_type=F32
-            )
-            acc[:, part] = product if block == 0 else acc[:, part] + product
+            product = probe_product(blocks, part)
+            acc[:, part] = product if 0 in blocks else acc[:, part] + product
             return carry
 
         lax.fori_loop(0, width // TILE, step, 0)
 
     def transpose_normed():
-        for copy in sent:
-            copy.wait_send()
-        sent.clear()
-
         def step(index, carry):
             part = span(index * 128, 128)
             w[0, part, 0:tokens] = normed[:, part].astype(F32).T.astype(BF16)
@@ -462,13 +558,17 @@
         lax.fori_loop(0, width // 128, step, 0)
 
     def forward():
+        drain(("w", "x", "d1", "d3"))
         for mask in everyone:
-            arrived("od", mask, o_at(mask, 1 - core))
+            arrived("ed", mask * PARTS, e_at(1 - core, mask, 0))
+            for part in range(PARTS):
+                arrived("fd", mask * PARTS + part, f_at(1 - core, mask, part))
 
         def step(index, carry):
             part = span(index * TILE, TILE)
-            product = jnp.dot(tctx[...], o[:, part], preferred_element_type=F32)
-            cot[:, part] = (product + acc[:, part] * query_width ** (-0.5)).astype(BF16)
+            total = jnp.dot(tctx[...], o[:, part], preferred_element_type=F32)
+            total = total + acc[:, part] * query_width ** (-0.5)
+            cot[:, part] = total.astype(BF16)
             return carry
 
         lax.fori_loop(0, width // TILE, step, 0)
@@ -514,7 +614,7 @@
             return carry
 
         lax.fori_loop(0, rows // chunk, step, 0)
-        return rows * wide * 1.5e-6
+        return rows * wide * 0.8e-6
 
     table = {}
     for name, base, wide, steps in streams:
@@ -532,20 +632,35 @@
         held = 1 if "x" in steps[:step] else 2
         kind = "%s%d" % (name, step)
         inbox = ref["rx_" + kind]
+        def still(got):
+            later = steps[step + 1 :]
+            return sum(1 for other in later if other == "x" or got & other) + (name == "v")
+
         if act == "x":
             slot = slots[name, step].index(mask)
-            push(kind, mask, home(name, mask, base + wide, wide), inbox.at[slot], across, slot)
-            plan.post("x", rows * wide * 2e-6 * US_PER_MB_ICI, lambda: land(name, step, mask))
+            source = home(name, mask, base + wide, wide)
+            plan.post(
+                "%s_%d" % (kind, mask),
+                "x",
+                size_mb(source) * US_PER_MB_ICI,
+                -still(mask),
+                lambda: push(kind, mask, source, inbox.at[slot], across, slot),
+                lambda: land(name, step, mask),
+            )
             waiting.add((step, mask))
             return 0.0
         if mask & act:
             got = mask ^ act
             slot = slots[name, step].index(got)
-            push(kind, mask, home(name, mask, base, held * wide), inbox.at[slot], along[act], slot)
+            source = home(name, mask, base, held * wide)
             plan.post(
+                "%s_%d" % (kind, got),
                 link_of(act),
-                ici_us(act, rows * held * wide * 2e-6),
+                size_mb(source) * US_PER_MB_ICI,
+                -still(got),
+                lambda: push(kind, mask, source, inbox.at[slot], along[act], slot),
                 lambda: land(name, step, got),
+                2.0 if act > 2 else 1.0,
             )
             return 0.0
         waiting.add((step, mask))
@@ -580,27 +695,25 @@
         us = add(lambda p: mine[p, :], lambda p: inbox[slot, p, :], write, held * wide)
         return us if last else us + ready(name, step + 1, mask)
 
-    def out_term(mask):
-        left_part = ctxt[shard_rows(mask), :]
-        target = slice(mask * rows, (mask + 1) * rows)
+    def out_term(masks):
+        left_part = jnp.concatenate([ctxt[shard_rows(mask), :] for mask in masks], axis=0)
         piece = q_part // 2
 
         def step(index, carry):
-            other, half, far = lax.div(index, 4), lax.rem(lax.div(index, 2), 2), lax.rem(index, 2)
-            mine_core, mine_far = lax.rem(pr, 2), lax.div(pr, 2)
-            block = (mine_far + far - 2 * mine_far * far) * 2 + (
-                mine_core + other - 2 * mine_core * other
-            )
-            columns = span(block * q_part + half * piece, piece)
-            sgn[target, span(index * piece, piece)] = jnp.dot(
-                left_part, cot[:, columns], preferred_element_type=F32
-            ).astype(BF16)
-            return carry
-
-        lax.fori_loop(0, width // piece, step, 0)
-        push("rd", mask, home("a", mask, 2 * q_part, 2 * q_part), ref["rxd"].at[mask], pair)
-
-        def met():
+            other, half = lax.div(index, 2), lax.rem(index, 2)
+            for far in range(2):
+                block = jnp.where(other == 0, block_of[2 * far], block_of[2 * far + 1])
+                columns = span(block * q_part + half * piece, piece)
+                product = jnp.dot(left_part, cot[:, columns], preferred_element_type=F32)
+                for place, mask in enumerate(masks):
+                    sgn[mask * rows : (mask + 1) * rows, span((2 * index + far) * piece, piece)] = (
+                        product[place * rows : (place + 1) * rows].astype(BF16)
+                    )
+            return carry
+
+        lax.fori_loop(0, width // piece // 2, step, 0)
+
+        def meet(mask):
             arrived("rd", mask, ref["rxd"].at[mask])
             mine = home("a", mask, 0, 2 * q_part)
 
@@ -611,15 +724,22 @@
             us += ready("b", 0, mask)
             return us + ready("a", 0, mask)
 
-        plan.post("pair", rows * 2 * q_part * 2e-6 * US_PER_MB_PAIR, met)
+        for mask in masks:
+            source = home("a", mask, 2 * q_part, 2 * q_part)
+            plan.post(
+                "rd_%d" % mask,
+                "pair",
+                size_mb(source) * US_PER_MB_PAIR,
+                0,
+                functools.partial(push, "rd", mask, source, ref["rxd"].at[mask], pair),
+                functools.partial(meet, mask),
+            )
 
     def value_term(mask):
         target = slice(mask * rows, (mask + 1) * rows)
         w[1, target, 0:key_width] = lax.dot_general(
             w[0, shard_rows(mask), 0:tokens], bvt[...], ROWS_BY_ROWS, preferred_element_type=F32
         ).astype(BF16)
-        push("rdv", mask, home("v", mask, 2 * k_part, 2 * k_part), ref["rxdv"].at[mask], pair)
-
         def met():
             arrived("rdv", mask, ref["rxdv"].at[mask])
             mine = home("v", mask, 0, 2 * k_part)
@@ -630,51 +750,79 @@
             us = add(lambda p: mine[p, :], lambda p: ref["rxdv"][mask, p, :], write, 2 * k_part)
             return us + ready("v", 0, mask)
 
-        plan.post("pair", rows * 2 * k_part * 2e-6 * US_PER_MB_PAIR, met)
-
-    plan.task("norm", 1.5, (), normalize)
-    for column in range(key_width // TILE):
+        source = home("v", mask, 2 * k_part, 2 * k_part)
+        plan.post(
+            "rv_%d" % mask,
+            "pair",
+            size_mb(source) * US_PER_MB_PAIR,
+            0,
+            lambda: push("rdv", mask, source, ref["rxdv"].at[mask], pair),
+            met,
+        )
+
+    columns_v = range(key_width // TILE)
+    plan.task("norm", 3.7, (), normalize)
+    for column in columns_v:
         plan.task("value_signs%d" % column, 1.3, (), functools.partial(value_signs, column))
-    sign_names = ["value_signs%d" % column for column in range(key_width // TILE)]
-    plan.task("tangent", 1.5, ["norm"] + sign_names, tangent)
+    needs = ["norm"] + ["value_signs%d" % column for column in columns_v]
+    plan.task("tangent", 1.3, needs, tangent)
     for part in range(sign_parts):
-        plan.task("out_signs%d" % part, 1.2, (), functools.partial(out_signs, part))
+        plan.task("out_signs%d" % part, 1.0, (), functools.partial(out_signs, part))
     sign_names = ["out_signs%d" % part for part in range(sign_parts)]
-    before = ["tangent"] + sign_names
-    for block in range(probes):
-        arrival = "all_w" if block < 2 else "all_x"
-        plan.task("project%d" % block, 2.5, before + [arrival], functools.partial(project, block))
-        plan.task("attend%d" % block, 4.2, ["project%d" % block], functools.partial(attend, block))
-        plan.task("probe%d" % block, 1.7, ["attend%d" % block], functools.partial(probe, block))
-        before = ["probe%d" % block]
-    plan.task("turn", 1.0, before + ["all_o"], transpose_normed)
-    plan.task("forward", 5.0, ["turn"], forward)
+    if rows % 128 == 0:
+        arrival_order = sorted(everyone, key=lambda mask: (bin(mask).count("1"), -low_bit(mask)))
+        groups = [[0] + arrival_order[:1]]
+        groups += [arrival_order[at : at + 2] for at in range(1, shards - 3, 2)]
+        groups += [arrival_order[-2:-1], arrival_order[-1:]]
+    else:
+        groups = [[]]
+    flags = ["w", "d1", "x", "d3"]
+    before = {0: ["tangent"], 1: ["tangent"], 2: ["attend0"], 3: ["attend1"]}
+    for pair_of in ((0, 1), (2, 3)):
+        for block in pair_of:
+            for index, group in enumerate(groups):
+                name = "shards%d_%d" % (block, index)
+                if group:
+                    arrivals = ["%s%d" % (flags[block], mask) for mask in group if mask]
+                    action = functools.partial(add_shards, block, group, index == 0)
+                else:
+                    arrivals = ["all_" + flags[block]]
+                    action = functools.partial(whole_project, block)
+                plan.task(name, 0.25 * len(group) + 0.47, before[block] + arrivals, action)
+                before[block] = [name]
+            name = "attend%d" % block
+            plan.task(name, 2.95, before[block] + ["tangent"], functools.partial(attend, block))
+        name = "probe%d" % pair_of[0]
+        needs = ["attend%d" % block for block in pair_of] + sign_names
+        plan.task(name, 3.8, needs, functools.partial(probe, pair_of))
+    needs = ["probe0", "probe2", "all_fd", "all_ed"]
+    plan.task("forward", 6.0, needs, forward)
     out_order = sorted(range(shards), key=lambda mask: [-(mask & bit) for bit in bits])
     value_order = sorted(range(shards), key=lambda mask: [-(mask & b) for b in bits[1:] + bits[:1]])
-    terms = [("out%d" % mask, 0.9, ("forward",), functools.partial(out_term, mask)) for mask in out_order]
+    terms = []
+    for at in range(0, shards, 2):
+        action = functools.partial(out_term, out_order[at : at + 2])
+        terms.append(("out%d" % at, 2.2, ("forward",), action))
     chain = []
     for block in range(probes):
         chain.append(("back%d" % block, 1.5, ("forward",), functools.partial(back_context, block)))
-        chain.append(
-            ("spread%d" % block, 1.0, ("back%d" % block,), functools.partial(spread_back, block))
-        )
-    spread_names = ["spread%d" % block for block in range(probes)]
+        action = functools.partial(spread_back, block)
+        chain.append(("spread%d" % block, 0.5, ("back%d" % block,), action))
+    chain.append(("turn", 1.5, ("forward", "all_x"), transpose_normed))
+    needs = ["turn"] + ["spread%d" % block for block in range(probes)]
     values = [
-        ("value%d" % mask, 0.2, spread_names, functools.partial(value_term, mask))
-        for mask in value_order
+        ("value%d" % mask, 0.3, needs, functools.partial(value_term, mask)) for mask in value_order
     ]
-    merged, early = [], 2
-    merged += terms[:early]
-    rest = terms[early:]
+    merged = terms[:1]
+    rest = terms[1:]
     while rest or chain:
-        merged += chain[:1]
+        merged += chain[:3]
         merged += rest[:1]
-        chain, rest = chain[1:], rest[1:]
+        chain, rest = chain[3:], rest[1:]
     for entry in merged + values:
         plan.task(*entry)
     plan.run()
-    for copy in sent:
-        copy.wait_send()
+    drain(list(sent))
 
 
 def body(hidden, norm_gain, query_weight, key_weight, value_weight, output_weight, probe_seed):

time: 185 us -> 160 us (0.86)
  Pallas kernels: 179 us -> 154 us
    pallas_call x1, Pallas kernels: 179 us -> 154 us  [body(): pl.pallas_call(functools.partial(kernel, sizes, list(scratch), streams, s...]
where the time goes in v1:
time: 160 us
  Pallas kernels  154 us (96%)
  local copies, waits for them, and re-layouts  4.73 us (3%)
    pallas_call x1, Pallas kernels, body(): pl.pallas_call(functools.partial(kernel, sizes, list(scratch), streams, s...  154 us
    unnamed x2, local copies, waits for them, and re-layouts  3.44 us

profile of v1, /device:TPU:0, one launch (start us, length us, event | category | flops | bytes accessed | tf_op | source)
XLA Modules:
  0.0 159.6 jit_solution(15237524652351468790)
XLA Ops:
  1.3 1.3 reshape.7.gain_ref
  2.6 153.6 %shard_map.104 = (f32[256,128]{1,0:T(8,128)}, f32[256,512]{1,0:T(8,128)}) custom-call(s32[1]{0:T(128)S(6)} %copy.13.seed_ref, bf16[1,2048]{1,0:T(2,128)(2,1)} %reshape.7.gain_ref, f32[256,128]{1,0:T(8,128)} %constant.4.clone.cos_ref, f32[256,128]{1,0:T(8,128)} %constant.5.clone.sin_ref, bf16[512,2048]{1,0:T(8,128)(2,1)} %hid_in.1, bf16[256,2048]{1,0:T(8,128)(2,1)} %q_in.1, ...), custom_call_target="tpu_custom_call" | custom-call | tf_op jit(solution)/shard_map/pallas_call | solution.py:839
  156.2 1.6 copy.14
  157.8 1.9 %copy.15 = f32[256,512]{1,0:T(8,128)} copy(f32[256,512]{1,0:T(8,128)} %get-tuple-element.5) | data formatting | bytes 1048576

commit v2 on v1

--- a/solution.py
+++ b/solution.py
@@ -32,6 +32,9 @@
 US_PER_MB_PAIR = 1.6
 LATENCY_US = 2.0
 AHEAD_US = 5.0
+FIRST_TERMS = 4
+CHAIN_STEP = 8
+TERM_STEP = 1
 PARTS = 2
 
 
@@ -141,9 +144,10 @@
     bits = bits_of(shards)
     near = bits[1:] if len(bits) > 1 else []
     streams = [
-        ("a", 0, q_part // 2, ["x"] + bits),
+        ("a", 0, q_part // 4, ["x"] + bits),
+        ("c", q_part // 2, q_part // 4, near + bits[:1] + ["x"]),
         ("b", q_part, q_part // 2, bits[:1] + ["x"] + near),
-        ("v", 0, k_part, near + bits[:1] + ["x"]),
+        ("v", 0, k_part, ["x"] + bits),
     ]
     vm = lambda shape, kind=BF16: pltpu.VMEM(shape, kind)
     sem = lambda count: pltpu.SemaphoreType.DMA((count,))
@@ -155,8 +159,7 @@
         "sgn": vm((query_width, width)),
         "att": vm((probes * (tokens // SEQ) * (q_part // HEAD_DIM), SEQ, SEQ)),
         "tv": vm((tokens, key_width)),
-        "raw": vm((2, tokens, q_part + 2 * k_part), F32),
-        "cblk": vm((probes, tokens, q_part)),
+        "raw": vm((probes, tokens, q_part + 2 * k_part), F32),
         "ctxt": vm((query_width, tokens)),
         "tctx": vm((tokens, query_width)),
         "acc": vm((tokens, width), F32),
@@ -187,10 +190,10 @@
     shards, tokens, width, query_width, key_width, probes = sizes
     ref = dict(zip(names, refs))
     w, o, hid, normed, sgn, att = (ref[n] for n in ("w", "o", "hid", "normed", "sgn", "att"))
-    tv, raw, cblk, ctxt, tctx, acc, bvt = (
-        ref[n] for n in ("tv", "raw", "cblk", "ctxt", "tctx", "acc", "bvt")
+    tv, raw, ctxt, tctx, acc, bvt = (
+        ref[n] for n in ("tv", "raw", "ctxt", "tctx", "acc", "bvt")
     )
-    cot = hid
+    context = cot = hid
     rows = width // shards
     q_part, k_part = query_width // probes, key_width // probes
     heads = q_part // HEAD_DIM
@@ -355,7 +358,7 @@
         if not first_wave and not second_wave:
             second_wave.append(True)
             for piece in range(PARTS):
-                start_f(0, piece, bits[1:])
+                start_f(0, piece)
             start_e(0, 0, bits[1:])
 
         def got_x():
@@ -390,8 +393,6 @@
         start_w(0, part)
     local[4].wait()
     start_e(0, 0, bits[:1])
-    for part in range(PARTS):
-        start_f(0, part, bits[:1])
 
     def normalize():
         local[3].wait()
@@ -460,7 +461,7 @@
     def project(block):
         def step(index, carry):
             part = span(index * TILE, TILE)
-            raw[block % 2, :, part] = jnp.dot(
+            raw[block, :, part] = jnp.dot(
                 normed[...], w[block, :, part], preferred_element_type=F32
             )
             return carry
@@ -490,7 +491,7 @@
             cut = [w[block, shard_rows(mask), part] for mask in masks]
             right_part = jnp.concatenate(cut, axis=0) if len(cut) > 1 else cut[0]
             product = jnp.dot(left_part, right_part, preferred_element_type=F32)
-            raw[block % 2, :, part] = product if first else raw[block % 2, :, part] + product
+            raw[block, :, part] = product if first else raw[block, :, part] + product
             return carry
 
         lax.fori_loop(0, (q_part + 2 * k_part) // TILE, step, 0)
@@ -509,12 +510,12 @@
             cosine, sine = cos_ref[...], sin_ref[...]
 
             def turned(low):
-                piece = raw[block % 2, part, low : low + HEAD_DIM]
+                piece = raw[block, part, low : low + HEAD_DIM]
                 other = pltpu.roll(piece, HEAD_DIM // 2, 1)
                 return (piece * cosine + other * sine).astype(BF16)
 
             key = turned(q_part)
-            value = raw[block % 2, part, q_part + k_part : q_part + 2 * k_part].astype(BF16)
+            value = raw[block, part, q_part + k_part : q_part + 2 * k_part].astype(BF16)
             both = jnp.concatenate([value, tv[part, span(there * k_part, k_part)]], axis=1)
             for head in range(heads):
                 low = head * HEAD_DIM
@@ -528,7 +529,7 @@
                 att[block * sequences * heads + sequence * heads + head] = weight
                 mixed = jnp.dot(weight, both, preferred_element_type=F32)
                 first = mixed[:, :HEAD_DIM]
-                cblk[block, part, low : low + HEAD_DIM] = first.astype(BF16)
+                context[part, block * q_part + low : block * q_part + low + HEAD_DIM] = first.astype(BF16)
                 ctxt[span(there * q_part + low, HEAD_DIM), part] = first.T.astype(BF16)
                 tctx[part, span(there * q_part + low, HEAD_DIM)] = mixed[:, HEAD_DIM:].astype(BF16)
             return carry
@@ -536,7 +537,7 @@
         lax.fori_loop(0, sequences, step, 0)
 
     def probe_product(blocks, part):
-        left_part = jnp.concatenate([cblk[block] for block in blocks], axis=1)
+        left_part = context[:, blocks[0] * q_part : (blocks[-1] + 1) * q_part]
         cut = [sgn[span(block_of[block] * q_part, q_part), part] for block in blocks]
         return jnp.dot(left_part, jnp.concatenate(cut, axis=0), preferred_element_type=F32)
 
@@ -552,26 +553,29 @@
     def transpose_normed():
         def step(index, carry):
             part = span(index * 128, 128)
-            w[0, part, 0:tokens] = normed[:, part].astype(F32).T.astype(BF16)
+            w[1, part, 0:tokens] = normed[:, part].astype(F32).T.astype(BF16)
             return carry
 
         lax.fori_loop(0, width // 128, step, 0)
 
-    def forward():
-        drain(("w", "x", "d1", "d3"))
-        for mask in everyone:
+    def forward(half):
+        if half:
+            drain(("w", "x", "d1", "d3"))
+        for mask in everyone if half else ():
             arrived("ed", mask * PARTS, e_at(1 - core, mask, 0))
             for part in range(PARTS):
                 arrived("fd", mask * PARTS + part, f_at(1 - core, mask, part))
 
+        piece = q_part // 2
+
         def step(index, carry):
-            part = span(index * TILE, TILE)
+            part = span((2 * index + half) * piece, piece)
             total = jnp.dot(tctx[...], o[:, part], preferred_element_type=F32)
             total = total + acc[:, part] * query_width ** (-0.5)
             cot[:, part] = total.astype(BF16)
             return carry
 
-        lax.fori_loop(0, width // TILE, step, 0)
+        lax.fori_loop(0, probes, step, 0)
 
     def back_context(block):
         def step(index, carry):
@@ -586,7 +590,7 @@
 
         lax.fori_loop(0, sequences, step, 0)
 
-    place_of = {0: 0, 2: 1, 1: 2, 3: 3}
+    place_of = {0: 0, 1: 1, 2: 2, 3: 3}
 
     def spread_back(block):
         def step(sequence, carry):
@@ -623,7 +627,7 @@
     def home(name, mask, low, wide):
         part = slice(mask * rows, (mask + 1) * rows)
         if name == "v":
-            return w.at[1, part, low : low + wide]
+            return w.at[0, part, low : low + wide]
         return sgn.at[part, low : low + wide]
 
     def ready(name, step, mask):
@@ -638,7 +642,7 @@
 
         if act == "x":
             slot = slots[name, step].index(mask)
-            source = home(name, mask, base + wide, wide)
+            source = home(name, mask, base + (2 * wide if name == "v" else wide), wide)
             plan.post(
                 "%s_%d" % (kind, mask),
                 "x",
@@ -647,7 +651,8 @@
                 lambda: push(kind, mask, source, inbox.at[slot], across, slot),
                 lambda: land(name, step, mask),
             )
-            waiting.add((step, mask))
+            if name != "v":
+                waiting.add((step, mask))
             return 0.0
         if mask & act:
             got = mask ^ act
@@ -687,78 +692,98 @@
                 mine[part, :] = total.astype(BF16)
             elif name == "v":
                 value_out[part, :] = total
-            elif name == "a":
-                output_out[part, 0:wide] = total
             else:
-                output_out[part, wide : 2 * wide] = total
+                output_out[part, base // 2 : base // 2 + wide] = total
 
         us = add(lambda p: mine[p, :], lambda p: inbox[slot, p, :], write, held * wide)
         return us if last else us + ready(name, step + 1, mask)
 
-    def out_term(masks):
+    def out_term(masks, half):
         left_part = jnp.concatenate([ctxt[shard_rows(mask), :] for mask in masks], axis=0)
-        piece = q_part // 2
-
-        def step(index, carry):
-            other, half = lax.div(index, 2), lax.rem(index, 2)
+        piece, quarter = q_part // 2, q_part // 4
+
+        def step(other, carry):
             for far in range(2):
                 block = jnp.where(other == 0, block_of[2 * far], block_of[2 * far + 1])
                 columns = span(block * q_part + half * piece, piece)
                 product = jnp.dot(left_part, cot[:, columns], preferred_element_type=F32)
                 for place, mask in enumerate(masks):
-                    sgn[mask * rows : (mask + 1) * rows, span((2 * index + far) * piece, piece)] = (
-                        product[place * rows : (place + 1) * rows].astype(BF16)
-                    )
-            return carry
-
-        lax.fori_loop(0, width // piece // 2, step, 0)
+                    target = slice(mask * rows, (mask + 1) * rows)
+                    part = product[place * rows : (place + 1) * rows].astype(BF16)
+                    if half:
+                        sgn[target, span(other * 2 * q_part + q_part + far * piece, piece)] = part
+                    else:
+                        low = other * 2 * q_part + far * quarter
+                        sgn[target, span(low, quarter)] = part[:, :quarter]
+                        sgn[target, span(low + 2 * quarter, quarter)] = part[:, quarter:]
+            return carry
+
+        lax.fori_loop(0, 2, step, 0)
+        low = half * q_part
 
         def meet(mask):
-            arrived("rd", mask, ref["rxd"].at[mask])
-            mine = home("a", mask, 0, 2 * q_part)
+            inbox = ref["rxd"].at[mask, :, low : low + q_part]
+            arrived("rd", mask * PARTS + half, inbox)
+            mine = home("a", mask, low, q_part)
 
             def write(part, total):
                 mine[part, :] = total.astype(BF16)
 
-            us = add(lambda p: mine[p, :], lambda p: ref["rxd"][mask, p, :], write, 2 * q_part)
-            us += ready("b", 0, mask)
-            return us + ready("a", 0, mask)
+            us = add(lambda p: mine[p, :], lambda p: inbox[p, :], write, q_part)
+            for name in ("b",) if half else ("c", "a"):
+                us += ready(name, 0, mask)
+            return us
 
         for mask in masks:
-            source = home("a", mask, 2 * q_part, 2 * q_part)
+            source = home("a", mask, 2 * q_part + low, q_part)
+            inbox = ref["rxd"].at[mask, :, low : low + q_part]
+            slot = mask * PARTS + half
             plan.post(
-                "rd_%d" % mask,
+                "rd%d_%d" % (half, mask),
                 "pair",
                 size_mb(source) * US_PER_MB_PAIR,
                 0,
-                functools.partial(push, "rd", mask, source, ref["rxd"].at[mask], pair),
+                functools.partial(push, "rd", slot, source, inbox, pair),
                 functools.partial(meet, mask),
             )
 
-    def value_term(mask):
-        target = slice(mask * rows, (mask + 1) * rows)
-        w[1, target, 0:key_width] = lax.dot_general(
-            w[0, shard_rows(mask), 0:tokens], bvt[...], ROWS_BY_ROWS, preferred_element_type=F32
+    def value_term(masks, group):
+        low = group * 2 * k_part
+        left_part = jnp.concatenate([w[1, shard_rows(mask), 0:tokens] for mask in masks], axis=0)
+        product = lax.dot_general(
+            left_part, bvt[low : low + 2 * k_part, :], ROWS_BY_ROWS, preferred_element_type=F32
         ).astype(BF16)
-        def met():
-            arrived("rdv", mask, ref["rxdv"].at[mask])
-            mine = home("v", mask, 0, 2 * k_part)
+        for place, mask in enumerate(masks):
+            target = slice(mask * rows, (mask + 1) * rows)
+            w[0, target, low : low + 2 * k_part] = product[place * rows : (place + 1) * rows]
+
+        def met(mask):
+            inbox = ref["rxdv"].at[mask, :, group * k_part : (group + 1) * k_part]
+            arrived("rdv", mask * PARTS + group, inbox)
+            mine = home("v", mask, low, k_part)
 
             def write(part, total):
                 mine[part, :] = total.astype(BF16)
 
-            us = add(lambda p: mine[p, :], lambda p: ref["rxdv"][mask, p, :], write, 2 * k_part)
-            return us + ready("v", 0, mask)
-
-        source = home("v", mask, 2 * k_part, 2 * k_part)
-        plan.post(
-            "rv_%d" % mask,
-            "pair",
-            size_mb(source) * US_PER_MB_PAIR,
-            0,
-            lambda: push("rdv", mask, source, ref["rxdv"].at[mask], pair),
-            met,
-        )
+            us = add(lambda p: mine[p, :], lambda p: inbox[p, :], write, k_part)
+            if group:
+                return us + ready("v", 0, mask)
+            table["v"][3].add((0, mask))
+            return us + combine("v", 0, mask)
+
+        for mask in masks:
+            source = home("v", mask, low + k_part, k_part)
+            inbox = ref["rxdv"].at[mask, :, group * k_part : (group + 1) * k_part]
+            plan.post(
+                "rv%d_%d" % (group, mask),
+                "pair",
+                size_mb(source) * US_PER_MB_PAIR,
+                0,
+                functools.partial(
+                    push, "rdv", mask * PARTS + group, source, inbox, pair
+                ),
+                functools.partial(met, mask),
+            )
 
     columns_v = range(key_width // TILE)
     plan.task("norm", 3.7, (), normalize)
@@ -777,7 +802,7 @@
     else:
         groups = [[]]
     flags = ["w", "d1", "x", "d3"]
-    before = {0: ["tangent"], 1: ["tangent"], 2: ["attend0"], 3: ["attend1"]}
+    before = {block: ["norm"] for block in range(probes)}
     for pair_of in ((0, 1), (2, 3)):
         for block in pair_of:
             for index, group in enumerate(groups):
@@ -795,31 +820,37 @@
         name = "probe%d" % pair_of[0]
         needs = ["attend%d" % block for block in pair_of] + sign_names
         plan.task(name, 3.8, needs, functools.partial(probe, pair_of))
+    needs = ["shards1_%d" % (len(groups) - 1)]
+    plan.task("turn", 1.7, needs, transpose_normed)
     needs = ["probe0", "probe2", "all_fd", "all_ed"]
-    plan.task("forward", 6.0, needs, forward)
-    out_order = sorted(range(shards), key=lambda mask: [-(mask & bit) for bit in bits])
-    value_order = sorted(range(shards), key=lambda mask: [-(mask & b) for b in bits[1:] + bits[:1]])
+    plan.task("forward1", 3.0, needs, functools.partial(forward, 1))
+    plan.task("forward0", 3.0, ["forward1", "out1_0"], functools.partial(forward, 0))
+    far_first = bits[2:] + bits[:2]
+    out_order = sorted(range(shards), key=lambda mask: [-(mask & bit) for bit in far_first])
+    value_order = sorted(range(shards), key=lambda mask: [-(mask & bit) for bit in bits])
     terms = []
     for at in range(0, shards, 2):
-        action = functools.partial(out_term, out_order[at : at + 2])
-        terms.append(("out%d" % at, 2.2, ("forward",), action))
+        for half in (1, 0):
+            action = functools.partial(out_term, out_order[at : at + 2], half)
+            terms.append(("out%d_%d" % (half, at), 1.1, ("forward%d" % half,), action))
     chain = []
-    for block in range(probes):
-        chain.append(("back%d" % block, 1.5, ("forward",), functools.partial(back_context, block)))
-        action = functools.partial(spread_back, block)
-        chain.append(("spread%d" % block, 0.5, ("back%d" % block,), action))
-    chain.append(("turn", 1.5, ("forward", "all_x"), transpose_normed))
-    needs = ["turn"] + ["spread%d" % block for block in range(probes)]
-    values = [
-        ("value%d" % mask, 0.3, needs, functools.partial(value_term, mask)) for mask in value_order
-    ]
-    merged = terms[:1]
-    rest = terms[1:]
+    for group, block_pair in ((1, (2, 3)), (0, (0, 1))):
+        for block in block_pair:
+            needs = ("forward0", "forward1")
+            chain.append(("back%d" % block, 1.5, needs, functools.partial(back_context, block)))
+            action = functools.partial(spread_back, block)
+            chain.append(("spread%d" % block, 0.5, ("back%d" % block,), action))
+        needs = ["turn"] + ["spread%d" % block for block in block_pair]
+        for at in range(0, shards, 2):
+            action = functools.partial(value_term, value_order[at : at + 2], group)
+            chain.append(("value%d_%d" % (group, at), 0.4, needs, action))
+    merged = terms[:FIRST_TERMS]
+    rest = terms[FIRST_TERMS:]
     while rest or chain:
-        merged += chain[:3]
-        merged += rest[:1]
-        chain, rest = chain[3:], rest[1:]
-    for entry in merged + values:
+        merged += chain[:CHAIN_STEP]
+        merged += rest[:TERM_STEP]
+        chain, rest = chain[CHAIN_STEP:], rest[TERM_STEP:]
+    for entry in merged:
         plan.task(*entry)
     plan.run()
     drain(list(sent))

time: 160 us -> 149 us (0.931)
  Pallas kernels: 154 us -> 143 us
    pallas_call x1, Pallas kernels: 154 us -> 143 us  [body(): pl.pallas_call(functools.partial(kernel, sizes, list(scratch), streams, s...]
where the time goes in v2:
time: 149 us
  Pallas kernels  143 us (96%)
  local copies, waits for them, and re-layouts  4.73 us (3%)
    pallas_call x1, Pallas kernels, body(): pl.pallas_call(functools.partial(kernel, sizes, list(scratch), streams, s...  143 us
    unnamed x2, local copies, waits for them, and re-layouts  3.44 us

profile of v2, /device:TPU:0, one launch (start us, length us, event | category | flops | bytes accessed | tf_op | source)
XLA Modules:
  0.0 148.8 jit_solution(1081771912071764667)
XLA Ops:
  1.3 1.3 reshape.7.gain_ref
  2.6 142.8 %shard_map.104 = (f32[256,128]{1,0:T(8,128)}, f32[256,512]{1,0:T(8,128)}) custom-call(s32[1]{0:T(128)S(6)} %copy.13.seed_ref, bf16[1,2048]{1,0:T(2,128)(2,1)} %reshape.7.gain_ref, f32[256,128]{1,0:T(8,128)} %constant.4.clone.cos_ref, f32[256,128]{1,0:T(8,128)} %constant.5.clone.sin_ref, bf16[512,2048]{1,0:T(8,128)(2,1)} %hid_in.1, bf16[256,2048]{1,0:T(8,128)(2,1)} %q_in.1, ...), custom_call_target="tpu_custom_call" | custom-call | tf_op jit(solution)/shard_map/pallas_call | solution.py:870
  145.4 1.6 %copy.14 = f32[256,128]{1,0:T(8,128)} copy(f32[256,128]{1,0:T(8,128)} %get-tuple-element.4) | data formatting | bytes 262144
  147.0 1.9 %copy.15 = f32[256,512]{1,0:T(8,128)} copy(f32[256,512]{1,0:T(8,128)} %get-tuple-element.5) | data formatting | bytes 1048576
